TPU v7x, 32 devices: a whole 2x2x4 slice. The times are simulated.
32 devices in a mesh: req: 2 (over y), blk: 4 (over z), uly: 4 (over x, core).
Axes of the slice: x: 2, y: 2, z: 4, core: 2. Of those that a mesh axis runs over, the one named last changes fastest.
Arguments:
- video_qkv: bfloat16 [3, 2048, 3072], P(None, ('req', 'blk', 'uly')), parts along dimension 1, may hold values from -16 to 16
- text_qkv: bfloat16 [3, 64, 3072], P(None, ('req', 'blk', 'uly')), parts along dimension 1, may hold values from -9.5625 to 9.5625
- video_gate: float32 [6144], P('req'), parts along dimension 0, may hold values from 1 to 4
- text_gate: float32 [6144], P('req'), parts along dimension 0, may hold values from 1 to 4
Outputs:
- video_out: bfloat16 [2048, 3072], P(('req', 'blk', 'uly')), parts along dimension 0
- text_out: bfloat16 [64, 3072], P(('req', 'blk', 'uly')), parts along dimension 0
There are 2 independent parts, one for each index of `req`. A program takes and returns all parts, laid end to end along the dimension named above; each array names one. Nothing has to cross between parts.
All inputs are finite; a program needn't handle non-finite values.
Results may differ from a plain program's by a relative error of at most 0.0085.
Values may be sent and summed in bfloat16 or wider, within the bound.
No kernel may reach another device: no remote copies, remote signals or barrier semaphores. Data moves between devices by JAX's collectives and lax.ppermute only.
A program may use at most 128 MiB of HBM per device.

v0:
```python
import math
import jax
import jax.numpy as jnp
from jax import lax
from jax.sharding import PartitionSpec as P

HEADS = 24
HD = 128


def merge_block(state, queries, block_pair):
    best, total, summed = state
    scale = 1.0 / math.sqrt(queries.shape[-1])
    scores = (
        jnp.einsum("qhd,khd->hqk", queries, block_pair[0], preferred_element_type=jnp.float32)
        * scale
    )
    new_best = jnp.maximum(best, jnp.max(scores, axis=2))
    factor = jnp.exp(best - new_best)
    raised = jnp.exp(scores - new_best[:, :, None])
    total = total * factor + jnp.sum(raised, axis=2)
    product = jnp.einsum(
        "hqk,khd->hqd",
        raised.astype(jnp.bfloat16),
        block_pair[1],
        preferred_element_type=jnp.float32,
    )
    summed = summed * factor[:, :, None] + product
    return (new_best, total, summed)


def attend(video_heads, text_heads):
    heads = video_heads.shape[3]
    width = video_heads.shape[4]
    rows_video = video_heads.shape[1]
    rows_text = text_heads.shape[1]
    joined = jnp.concatenate((video_heads, text_heads), axis=1)
    rows_all = rows_video + rows_text
    joined = joined.reshape(3, rows_all, heads, width)
    queries = joined[0]
    key_pairs = joined[1:]
    initial = (
        jnp.full((heads, rows_all), -jnp.inf, jnp.float32),
        jnp.zeros((heads, rows_all), jnp.float32),
        jnp.zeros((heads, rows_all, width), jnp.float32),
    )
    piece = lax.all_gather(key_pairs, "blk", axis=1, tiled=True)
    count = piece.shape[1] // rows_all

    def one_block(index, inner):
        block_pair = lax.dynamic_slice_in_dim(piece, index * rows_all, rows_all, 1)
        return merge_block(inner, queries, block_pair)

    best, total, summed = lax.fori_loop(0, count, one_block, initial)
    attended = (summed / total[:, :, None]).transpose(1, 0, 2).astype(jnp.bfloat16)
    video_att = attended[:rows_video].reshape(rows_video, 1, heads, width)
    text_att = attended[rows_video:].reshape(rows_text, 1, heads, width)
    return (video_att, text_att)


def on_device(video_qkv, text_qkv, video_gate, text_gate):
    groups = lax.axis_size("uly")
    local_heads = HEADS // groups
    video_rows = video_qkv.shape[1]
    text_rows = text_qkv.shape[1]
    video_split = video_qkv.reshape(3, video_rows, groups, local_heads, HD)
    text_split = text_qkv.reshape(3, text_rows, groups, local_heads, HD)
    video_heads, text_heads = (
        lax.all_to_all(video_split, "uly", split_axis=2, concat_axis=1, tiled=True),
        lax.all_to_all(text_split, "uly", split_axis=2, concat_axis=1, tiled=True),
    )
    video_att, text_att = attend(video_heads, text_heads)
    video_back, text_back = (
        lax.all_to_all(video_att, "uly", split_axis=0, concat_axis=1, tiled=True),
        lax.all_to_all(text_att, "uly", split_axis=0, concat_axis=1, tiled=True),
    )
    video_flat = video_back.reshape(video_rows, HEADS * HD).astype(jnp.float32)
    text_flat = text_back.reshape(text_rows, HEADS * HD).astype(jnp.float32)
    video_out = (video_flat * video_gate[None, :]).astype(jnp.bfloat16)
    text_out = (text_flat * text_gate[None, :]).astype(jnp.bfloat16)
    return (video_out, text_out)


def solution(mesh):
    in_specs = (
        P(None, ("req", "blk", "uly"), None),
        P(None, ("req", "blk", "uly"), None),
        P("req"),
        P("req"),
    )
    out_specs = (P(("req", "blk", "uly"), None), P(("req", "blk", "uly"), None))
    return jax.shard_map(
        on_device, mesh=mesh, in_specs=in_specs, out_specs=out_specs, check_vma=False
    )
```

profile of v0, /device:TPU:0, one launch (start us, length us, event | category | flops | bytes accessed | tf_op | source)
XLA Modules:
  0.0 148.8 jit_solution(10764639887761051975)
XLA Ops:
  7.2 0.8 reshape.38
  8.0 0.6 copy.22
  8.6 4.2 %all-to-all-start.1 = ((bf16[3,2,4,6,128]{4,1,3,0,2:T(2,128)(2,1)}), bf16[3,2,4,6,128]{4,1,3,0,2:T(2,128)(2,1)S(1)}, u32[]{:S(2)}, u32[]{:S(2)}) async-start(bf16[3,2,4,6,128]{4,1,3,0,2:T(2,128)(2,1)} %copy.22), calls=%async_computation.1 | async-start | bytes 73728 | tf_op jit(solution)/shard_map/all_to_all | solution.py:70
  12.9 2.8 %reshape.37 = bf16[3,64,4,6,128]{4,3,2,1,0:T(8,128)(2,1)S(1)} reshape(bf16[3,64,3072]{2,1,0:T(8,128)(2,1)} %param.6) | data formatting | bytes 2359296 | tf_op jit(solution)/shard_map/reshape | solution.py:66
  15.7 1.5 copy.20
  17.2 0.0 all-to-all-done.1
  17.2 3.5 %all-to-all-start = ((bf16[3,64,4,6,128]{4,1,3,0,2:T(8,128)(2,1)}), bf16[3,64,4,6,128]{4,1,3,0,2:T(8,128)(2,1)S(1)}, u32[]{:S(2)}, u32[]{:S(2)}) async-start(bf16[3,64,4,6,128]{4,1,3,0,2:T(8,128)(2,1)} %copy.20), calls=%async_computation | async-start | bytes 2359296 | tf_op jit(solution)/shard_map/all_to_all | solution.py:69
  20.7 0.0 all-gather.3.cloned.1.call-start
  20.8 15.7 %all-to-all-done = bf16[3,64,4,6,128]{4,1,3,0,2:T(8,128)(2,1)S(1)} async-done(((bf16[3,64,4,6,128]{4,1,3,0,2:T(8,128)(2,1)}), bf16[3,64,4,6,128]{4,1,3,0,2:T(8,128)(2,1)S(1)}, u32[]{:S(2)}, u32[]{:S(2)}) %all-to-all-start) | async-done | bytes 1179680 | tf_op jit(solution)/shard_map/all_to_all | solution.py:69
  36.5 0.1 copy.21
  36.6 1.0 fusion.12
  37.6 0.0 all-gather.3.cloned.1.call-update
  37.7 66.0 %all-gather.3.cloned.1.call-done = bf16[2,1056,1,6,128]{4,1,3,0,2:T(8,128)(2,1)} async-done(((bf16[2,264,1,6,128]{4,1,3,0,2:T(8,128)(2,1)}), bf16[2,1056,1,6,128]{4,1,3,0,2:T(8,128)(2,1)}) %all-gather.3.cloned.1.call-update) | async-done | bytes 3244048 | tf_op jit(solution)/shard_map/all_gather | solution.py:47
  103.7 16.6 %while.18 = (s32[]{:T(128)}, f32[6,264]{1,0:T(8,128)S(1)}, f32[6,264]{1,0:T(8,128)S(1)}, f32[6,264,128]{2,1,0:T(8,128)S(1)}, bf16[2,1056,6,128]{3,1,2,0:T(8,128)...) while((s32[]{:T(128)}, f32[6,264]{1,0:T(8,128)S(1)}, ...), condition=%wide.region_3.0_spmd.clone, body=%wide.region_0.0_spmd.clone.sunk | while | flops 218067712 | bytes 7958215 | solution.py:54
  103.7 1.6 %bitcast_reduce_fusion.2 = (f32[6,264]{1,0:T(8,128)S(1)}, f32[6,264,264]{2,1,0:T(8,128)S(1)}) fusion(bf16[264,6,128]{2,0,1:T(8,128)(2,1)S(1)} %get-tuple-element.223, bf16[2,1056,6,128]{3,1,2,0:T(8,128)(2,1)} %get-tuple-element.222, s32[]{:T(128)S(6)} %select_n.9), kind=kOutput, calls=%fused_computation.1.clone.1 | convolution fusion | flops 107887824 | bytes 2490052 | tf_op jit(solution)/shard_map/while/body/eval_jaxpr/qhd,khd->hqk/dot_general | solution.py:15
  105.3 0.4 fusion.24
  105.8 2.0 %convolution_add_fusion.2 = f32[6,264,128]{2,1,0:T(8,128)S(1)} fusion(f32[6,264,264]{2,1,0:T(8,128)S(1)} %get-tuple-element.193, f32[6,264]{1,0:T(8,128)S(1)} %select_maximum_fusion.2, f32[6,264,128]{2,1,0:T(8,128)S(1)} %get-tuple-element.210, bf16[2,1056,6,128]{3,1,2,0:T(8,128)(2,1)} %get-tuple-element.222, s32[]{:T(128)S(6)} %add.53, ...), kind=kOutput, calls=%fused_computation.5.clone.1 | convolution fusion | flops 108915840 | bytes 3712905 | tf_op jit(solution)/shard_map/while/body/eval_jaxpr/hqk,khd->hqd/dot_general | solution.py:22
  107.8 1.6 %bitcast_reduce_fusion.2 = (f32[6,264]{1,0:T(8,128)S(1)}, f32[6,264,264]{2,1,0:T(8,128)S(1)}) fusion(bf16[264,6,128]{2,0,1:T(8,128)(2,1)S(1)} %get-tuple-element.223, bf16[2,1056,6,128]{3,1,2,0:T(8,128)(2,1)} %get-tuple-element.222, s32[]{:T(128)S(6)} %select_n.9), kind=kOutput, calls=%fused_computation.1.clone.1 | convolution fusion | flops 107887824 | bytes 2490052 | tf_op jit(solution)/shard_map/while/body/eval_jaxpr/qhd,khd->hqk/dot_general | solution.py:15
  109.5 0.4 fusion.24
  109.9 2.0 %convolution_add_fusion.2 = f32[6,264,128]{2,1,0:T(8,128)S(1)} fusion(f32[6,264,264]{2,1,0:T(8,128)S(1)} %get-tuple-element.193, f32[6,264]{1,0:T(8,128)S(1)} %select_maximum_fusion.2, f32[6,264,128]{2,1,0:T(8,128)S(1)} %get-tuple-element.210, bf16[2,1056,6,128]{3,1,2,0:T(8,128)(2,1)} %get-tuple-element.222, s32[]{:T(128)S(6)} %add.53, ...), kind=kOutput, calls=%fused_computation.5.clone.1 | convolution fusion | flops 108915840 | bytes 3712905 | tf_op jit(solution)/shard_map/while/body/eval_jaxpr/hqk,khd->hqd/dot_general | solution.py:22
  112.0 1.6 %bitcast_reduce_fusion.2 = (f32[6,264]{1,0:T(8,128)S(1)}, f32[6,264,264]{2,1,0:T(8,128)S(1)}) fusion(bf16[264,6,128]{2,0,1:T(8,128)(2,1)S(1)} %get-tuple-element.223, bf16[2,1056,6,128]{3,1,2,0:T(8,128)(2,1)} %get-tuple-element.222, s32[]{:T(128)S(6)} %select_n.9), kind=kOutput, calls=%fused_computation.1.clone.1 | convolution fusion | flops 107887824 | bytes 2490052 | tf_op jit(solution)/shard_map/while/body/eval_jaxpr/qhd,khd->hqk/dot_general | solution.py:15
  113.6 0.4 fusion.24
  114.1 2.0 %convolution_add_fusion.2 = f32[6,264,128]{2,1,0:T(8,128)S(1)} fusion(f32[6,264,264]{2,1,0:T(8,128)S(1)} %get-tuple-element.193, f32[6,264]{1,0:T(8,128)S(1)} %select_maximum_fusion.2, f32[6,264,128]{2,1,0:T(8,128)S(1)} %get-tuple-element.210, bf16[2,1056,6,128]{3,1,2,0:T(8,128)(2,1)} %get-tuple-element.222, s32[]{:T(128)S(6)} %add.53, ...), kind=kOutput, calls=%fused_computation.5.clone.1 | convolution fusion | flops 108915840 | bytes 3712905 | tf_op jit(solution)/shard_map/while/body/eval_jaxpr/hqk,khd->hqd/dot_general | solution.py:22
  116.2 1.6 %bitcast_reduce_fusion.2 = (f32[6,264]{1,0:T(8,128)S(1)}, f32[6,264,264]{2,1,0:T(8,128)S(1)}) fusion(bf16[264,6,128]{2,0,1:T(8,128)(2,1)S(1)} %get-tuple-element.223, bf16[2,1056,6,128]{3,1,2,0:T(8,128)(2,1)} %get-tuple-element.222, s32[]{:T(128)S(6)} %select_n.9), kind=kOutput, calls=%fused_computation.1.clone.1 | convolution fusion | flops 107887824 | bytes 2490052 | tf_op jit(solution)/shard_map/while/body/eval_jaxpr/qhd,khd->hqk/dot_general | solution.py:15
  117.8 0.4 fusion.24
  118.3 2.0 %convolution_add_fusion.2 = f32[6,264,128]{2,1,0:T(8,128)S(1)} fusion(f32[6,264,264]{2,1,0:T(8,128)S(1)} %get-tuple-element.193, f32[6,264]{1,0:T(8,128)S(1)} %select_maximum_fusion.2, f32[6,264,128]{2,1,0:T(8,128)S(1)} %get-tuple-element.210, bf16[2,1056,6,128]{3,1,2,0:T(8,128)(2,1)} %get-tuple-element.222, s32[]{:T(128)S(6)} %add.53, ...), kind=kOutput, calls=%fused_computation.5.clone.1 | convolution fusion | flops 108915840 | bytes 3712905 | tf_op jit(solution)/shard_map/while/body/eval_jaxpr/hqk,khd->hqd/dot_general | solution.py:22
  120.3 0.0 copy-start.1
  120.3 0.1 copy.24
  120.5 0.4 fusion.13
  120.8 0.6 slice_bitcast_fusion.1
  121.4 3.3 %all-to-all-start.3 = ((bf16[8,1,6,128]{3,2,1,0:T(8,128)(2,1)}), bf16[8,1,6,128]{3,2,1,0:T(8,128)(2,1)S(1)}, u32[]{:S(2)}, u32[]{:S(2)}) async-start(bf16[8,1,6,128]{3,2,1,0:T(8,128)(2,1)} %slice_bitcast_fusion.1), calls=%async_computation.3 | async-start | bytes 32768 | tf_op jit(solution)/shard_map/all_to_all | solution.py:75
  124.7 0.8 slice_bitcast_fusion
  125.5 0.0 copy-start
  125.5 3.0 %all-to-all-done.3 = bf16[8,1,6,128]{3,2,1,0:T(8,128)(2,1)S(1)} async-done(((bf16[8,1,6,128]{3,2,1,0:T(8,128)(2,1)}), bf16[8,1,6,128]{3,2,1,0:T(8,128)(2,1)S(1)}, u32[]{:S(2)}, u32[]{:S(2)}) %all-to-all-start.3) | async-done | bytes 12320 | tf_op jit(solution)/shard_map/all_to_all | solution.py:75
  128.5 3.5 %all-to-all-start.2 = ((bf16[256,1,6,128]{3,2,1,0:T(8,128)(2,1)}), bf16[256,1,6,128]{3,2,1,0:T(8,128)(2,1)S(1)}, u32[]{:S(2)}, u32[]{:S(2)}) async-start(bf16[256,1,6,128]{3,2,1,0:T(8,128)(2,1)} %slice_bitcast_fusion), calls=%async_computation.2 | async-start | bytes 1048576 | tf_op jit(solution)/shard_map/all_to_all | solution.py:74
  132.0 0.0 copy-done.1
  132.0 0.6 multiply_convert_fusion.1
  132.7 8.1 %all-to-all-done.2 = bf16[256,1,6,128]{3,2,1,0:T(8,128)(2,1)S(1)} async-done(((bf16[256,1,6,128]{3,2,1,0:T(8,128)(2,1)}), bf16[256,1,6,128]{3,2,1,0:T(8,128)(2,1)S(1)}, u32[]{:S(2)}, u32[]{:S(2)}) %all-to-all-start.2) | async-done | bytes 393248 | tf_op jit(solution)/shard_map/all_to_all | solution.py:74
  140.8 0.1 copy_bitcast_fusion
  140.9 0.2 reshape.41
  141.1 0.0 copy-done
  141.1 0.8 multiply_convert_fusion
  (19 shorter events, 0.2 us)
Async XLA Ops:
  8.6 8.6 %all-to-all-start.1 = ((bf16[3,2,4,6,128]{4,1,3,0,2:T(2,128)(2,1)}), bf16[3,2,4,6,128]{4,1,3,0,2:T(2,128)(2,1)S(1)}, u32[]{:S(2)}, u32[]{:S(2)}) async-start(bf16[3,2,4,6,128]{4,1,3,0,2:T(2,128)(2,1)} %copy.22), calls=%async_computation.1 | async-start | bytes 73728 | tf_op jit(solution)/shard_map/all_to_all | solution.py:70
  17.2 19.3 %all-to-all-start = ((bf16[3,64,4,6,128]{4,1,3,0,2:T(8,128)(2,1)}), bf16[3,64,4,6,128]{4,1,3,0,2:T(8,128)(2,1)S(1)}, u32[]{:S(2)}, u32[]{:S(2)}) async-start(bf16[3,64,4,6,128]{4,1,3,0,2:T(8,128)(2,1)} %copy.20), calls=%async_computation | async-start | bytes 2359296 | tf_op jit(solution)/shard_map/all_to_all | solution.py:69
  20.7 83.0 %all-gather.3.cloned.1.call-start = ((), (), s32[]{:S(2)}) async-start(), calls=%async_computation.4 | async-start | bytes 4055040 | tf_op jit(solution)/shard_map/all_gather | solution.py:47
  120.3 11.7 %copy-start.1 = (f32[3072]{0:T(1024)S(1)}, f32[3072]{0:T(1024)}, u32[]{:S(2)}) copy-start(f32[3072]{0:T(1024)} %param.9) | copy-start | bytes 36868
  121.4 7.1 %all-to-all-start.3 = ((bf16[8,1,6,128]{3,2,1,0:T(8,128)(2,1)}), bf16[8,1,6,128]{3,2,1,0:T(8,128)(2,1)S(1)}, u32[]{:S(2)}, u32[]{:S(2)}) async-start(bf16[8,1,6,128]{3,2,1,0:T(8,128)(2,1)} %slice_bitcast_fusion.1), calls=%async_computation.3 | async-start | bytes 32768 | tf_op jit(solution)/shard_map/all_to_all | solution.py:75
  125.5 15.6 %copy-start = (f32[3072]{0:T(1024)S(1)}, f32[3072]{0:T(1024)}, u32[]{:S(2)}) copy-start(f32[3072]{0:T(1024)} %param.8) | copy-start | bytes 36868
  128.5 12.3 %all-to-all-start.2 = ((bf16[256,1,6,128]{3,2,1,0:T(8,128)(2,1)}), bf16[256,1,6,128]{3,2,1,0:T(8,128)(2,1)S(1)}, u32[]{:S(2)}, u32[]{:S(2)}) async-start(bf16[256,1,6,128]{3,2,1,0:T(8,128)(2,1)} %slice_bitcast_fusion), calls=%async_computation.2 | async-start | bytes 1048576 | tf_op jit(solution)/shard_map/all_to_all | solution.py:74
Sparse Core Ops, SparseCore 0:
  37.7 65.8 all-gather.2
where the time goes:
time: 150 us; the launch traced here: 149 us
  waiting for transfers between devices  92.8 us (62%)
  starting transfers between devices  14.5 us (10%)
  matrix products  14.5 us (10%)
  between operations  14.2 us (9%)
  local copies, waits for them, and re-layouts  7.71 us (5%)
  other arithmetic  4.76 us (3%)
    all_gather x1, waiting for transfers between devices, attend(): piece = lax.all_gather(key_pairs, 'blk', axis=1, tiled=True)  66 us
    all_to_all x1, waiting for transfers between devices, on_device(): lax.all_to_all(video_split, 'uly', split_axis=2, concat_axis=1, tiled=True)  15.7 us
    all_to_all x1, waiting for transfers between devices, on_device(): lax.all_to_all(video_att, 'uly', split_axis=0, concat_axis=1, tiled=True)  8.12 us
    dot_general x4, matrix products, merge_block(): jnp.einsum('hqk,khd->hqd', raised.astype(jnp.bfloat16), block_pair[1], pr...  8.08 us
    dot_general x4, matrix products, merge_block(): jnp.einsum('qhd,khd->hqk', queries, block_pair[0], preferred_element_type...  6.46 us
    reshape x2, local copies, waits for them, and re-layouts, on_device(): video_split = video_qkv.reshape(3, video_rows, groups, local_heads, HD)  4.32 us
    all_to_all x1, starting transfers between devices, on_device(): lax.all_to_all(text_split, 'uly', split_axis=2, concat_axis=1, tiled=True)  4.24 us
    all_to_all x1, starting transfers between devices, on_device(): lax.all_to_all(video_split, 'uly', split_axis=2, concat_axis=1, tiled=True)  3.53 us
  transfers between devices with their start and end apart: 5, of which 4 were waited for; matrix products, arithmetic and copies ran while one was open for 4% of the time, Pallas kernels for 0%

commit v1 on v0

--- a/solution.py
+++ b/solution.py
@@ -6,6 +6,19 @@
 
 HEADS = 24
 HD = 128
+
+
+def gather_around(x, axis, dim):
+    devices, mine, rows = (lax.axis_size(axis), lax.axis_index(axis), x.shape[dim])
+    upward = [(i, (i + 1) % devices) for i in range(devices)]
+    result = jnp.zeros((*x.shape[:dim], devices * rows, *x.shape[dim + 1 :]), x.dtype)
+    current = x
+    for step in range(devices):
+        owner = (mine - step) % devices
+        result = lax.dynamic_update_slice_in_dim(result, current, owner * rows, axis=dim)
+        if step < devices - 1:
+            current = lax.ppermute(current, axis, upward)
+    return result
 
 
 def merge_block(state, queries, block_pair):
@@ -44,7 +57,7 @@
         jnp.zeros((heads, rows_all), jnp.float32),
         jnp.zeros((heads, rows_all, width), jnp.float32),
     )
-    piece = lax.all_gather(key_pairs, "blk", axis=1, tiled=True)
+    piece = gather_around(key_pairs, "blk", 1)
     count = piece.shape[1] // rows_all
 
     def one_block(index, inner):

time: 150 us -> 138 us (0.920)
  between operations: 14.2 us -> 0.79 us
  waiting for transfers between devices: 92.8 us -> 83.6 us
  local copies, waits for them, and re-layouts: 7.71 us -> 15.2 us
  starting transfers between devices: 14.5 us -> 16.6 us
    all_gather x1 -> x0, waiting for transfers between devices: 66 us -> none  [attend(): piece = lax.all_gather(key_pairs, 'blk', axis=1, tiled=True)]
    ppermute x0 -> x3, waiting for transfers between devices: none -> 56.8 us  [gather_around(): current = lax.ppermute(current, axis, upward)]
    dynamic_update_slice x0 -> x3, local copies, waits for them, and re-layouts: none -> 5.43 us  [gather_around(): lax.dynamic_update_slice_in_dim(result, current, owner * rows, axis=dim)]
    ppermute x0 -> x3, starting transfers between devices: none -> 2.12 us  [gather_around(): current = lax.ppermute(current, axis, upward)]
    broadcast_in_dim x0 -> x1, local copies, waits for them, and re-layouts: none -> 2.1 us  [gather_around(): jnp.zeros((*x.shape[:dim], devices * rows, *x.shape[dim + 1:]), x.dtype)]
  transfers between devices with their start and end apart: 5 -> 7, of which waited for: 4 -> 6; matrix products, arithmetic and copies ran while one was open for 4% -> 7% of each run, Pallas kernels for 0% -> 0%
where the time goes in v1:
time: 138 us; the launch traced here: 137 us
  waiting for transfers between devices  83.6 us (61%)
  starting transfers between devices  16.6 us (12%)
  local copies, waits for them, and re-layouts  15.2 us (11%)
  matrix products  15 us (11%)
  other arithmetic  5.67 us (4%)
    ppermute x3, waiting for transfers between devices, gather_around(): current = lax.ppermute(current, axis, upward)  56.8 us
    all_to_all x1, waiting for transfers between devices, on_device(): lax.all_to_all(video_split, 'uly', split_axis=2, concat_axis=1, tiled=True)  15.7 us
    all_to_all x1, waiting for transfers between devices, on_device(): lax.all_to_all(video_att, 'uly', split_axis=0, concat_axis=1, tiled=True)  8.12 us
    dot_general x4, matrix products, merge_block(): jnp.einsum('hqk,khd->hqd', raised.astype(jnp.bfloat16), block_pair[1], pr...  8.08 us
    dot_general x4, matrix products, merge_block(): jnp.einsum('qhd,khd->hqk', queries, block_pair[0], preferred_element_type...  6.91 us
    dynamic_update_slice x3, local copies, waits for them, and re-layouts, gather_around(): lax.dynamic_update_slice_in_dim(result, current, owner * rows, axis=dim)  5.43 us
    reshape x2, local copies, waits for them, and re-layouts, on_device(): video_split = video_qkv.reshape(3, video_rows, groups, local_heads, HD)  4.32 us
    all_to_all x1, starting transfers between devices, on_device(): lax.all_to_all(text_split, 'uly', split_axis=2, concat_axis=1, tiled=True)  4.24 us
  transfers between devices with their start and end apart: 7, of which 6 were waited for; matrix products, arithmetic and copies ran while one was open for 7% of the time, Pallas kernels for 0%

profile of v1, /device:TPU:0, one launch (start us, length us, event | category | flops | bytes accessed | tf_op | source)
XLA Modules:
  0.0 137.1 jit_solution(18054635838747636413)
XLA Ops:
  0.6 0.8 reshape.38
  1.4 0.6 copy.22
  2.1 4.2 %all-to-all-start.1 = ((bf16[3,2,4,6,128]{4,1,3,0,2:T(2,128)(2,1)}), bf16[3,2,4,6,128]{4,1,3,0,2:T(2,128)(2,1)S(1)}, u32[]{:S(2)}, u32[]{:S(2)}) async-start(bf16[3,2,4,6,128]{4,1,3,0,2:T(2,128)(2,1)} %copy.22), calls=%async_computation.1 | async-start | bytes 73728 | tf_op jit(solution)/shard_map/all_to_all | solution.py:83
  6.3 2.8 %reshape.37 = bf16[3,64,4,6,128]{4,3,2,1,0:T(8,128)(2,1)S(1)} reshape(bf16[3,64,3072]{2,1,0:T(8,128)(2,1)} %param.6) | data formatting | bytes 2359296 | tf_op jit(solution)/shard_map/reshape | solution.py:79
  9.2 1.5 %copy.20 = bf16[3,64,4,6,128]{4,1,3,0,2:T(8,128)(2,1)} copy(bf16[3,64,4,6,128]{4,3,2,1,0:T(8,128)(2,1)S(1)} %reshape.37) | data formatting | bytes 2359296 | tf_op jit(solution)/shard_map/reshape | solution.py:79
  10.6 0.0 all-to-all-done.1
  10.6 3.5 %all-to-all-start = ((bf16[3,64,4,6,128]{4,1,3,0,2:T(8,128)(2,1)}), bf16[3,64,4,6,128]{4,1,3,0,2:T(8,128)(2,1)S(1)}, u32[]{:S(2)}, u32[]{:S(2)}) async-start(bf16[3,64,4,6,128]{4,1,3,0,2:T(8,128)(2,1)} %copy.20), calls=%async_computation | async-start | bytes 2359296 | tf_op jit(solution)/shard_map/all_to_all | solution.py:82
  14.2 15.7 %all-to-all-done = bf16[3,64,4,6,128]{4,1,3,0,2:T(8,128)(2,1)S(1)} async-done(((bf16[3,64,4,6,128]{4,1,3,0,2:T(8,128)(2,1)}), bf16[3,64,4,6,128]{4,1,3,0,2:T(8,128)(2,1)S(1)}, u32[]{:S(2)}, u32[]{:S(2)}) %all-to-all-start) | async-done | bytes 1179680 | tf_op jit(solution)/shard_map/all_to_all | solution.py:82
  30.0 0.1 copy.21
  30.1 2.1 %broadcast_in_dim.24 = bf16[2,1056,6,128]{3,1,2,0:T(8,128)(2,1)} broadcast(bf16[]{:T(256)} %constant.87.clone.1), dimensions={} | broadcast | bytes 3244034 | tf_op jit(solution)/shard_map/broadcast_in_dim | solution.py:14
  32.2 1.1 constant_dynamic-update-slice_fusion.3
  33.3 2.1 %collective-permute-start = (bf16[2,264,6,128]{3,1,2,0:T(8,128)(2,1)S(1)}, bf16[2,264,6,128]{3,1,2,0:T(8,128)(2,1)S(1)}, u32[]{:S(2)}, u32[]{:S(2)}) collective-permute-start(bf16[2,264,6,128]{3,1,2,0:T(8,128)(2,1)S(1)} %get-tuple-element.150), channel_id=1, source_target_pairs={{0,4},{4,8},{8,12},{12,0},{1,5},{5,9},{9,13},{13,1},{2,6},{6,10},{... | collective-permute-start | bytes 2433032 | tf_op jit(solution)/shard_map/ppermute | solution.py:20
  35.4 19.8 %collective-permute-done = bf16[2,264,6,128]{3,1,2,0:T(8,128)(2,1)S(1)} collective-permute-done((bf16[2,264,6,128]{3,1,2,0:T(8,128)(2,1)S(1)}, bf16[2,264,6,128]{3,1,2,0:T(8,128)(2,1)S(1)}, u32[]{:S(2)}, u32[]{:S(2)}) %collective-permute-start) | collective-permute-done | bytes 811040 | tf_op jit(solution)/shard_map/ppermute | solution.py:20
  55.2 0.0 collective-permute-start.1
  55.2 20.8 %collective-permute-done.1 = bf16[2,264,6,128]{3,1,2,0:T(8,128)(2,1)} collective-permute-done((bf16[2,264,6,128]{3,1,2,0:T(8,128)(2,1)S(1)}, bf16[2,264,6,128]{3,1,2,0:T(8,128)(2,1)}, u32[]{:S(2)}, u32[]{:S(2)}) %collective-permute-start.1) | collective-permute-done | bytes 811040 | tf_op jit(solution)/shard_map/ppermute | solution.py:20
  76.0 0.0 collective-permute-start.2
  76.0 0.8 fusion.15
  76.8 1.0 constant_dynamic-update-slice_fusion.2
  77.9 2.2 %constant_dynamic-update-slice_fusion.1 = bf16[2,1056,6,128]{3,1,2,0:T(8,128)(2,1)} fusion(bf16[2,1056,6,128]{3,1,2,0:T(8,128)(2,1)} %constant_dynamic-update-slice_fusion.2, bf16[2,264,6,128]{3,1,2,0:T(8,128)(2,1)} %collective-permute-done.1, s32[]{:T(128)S(6)} %select_n.43), kind=kLoop, calls=%fused_computation.35 | loop fusion | bytes 1622020 | tf_op jit(solution)/shard_map/dynamic_update_slice | solution.py:18
  80.1 16.1 %collective-permute-done.2 = bf16[2,264,6,128]{3,1,2,0:T(8,128)(2,1)} collective-permute-done((bf16[2,264,6,128]{3,1,2,0:T(8,128)(2,1)}, bf16[2,264,6,128]{3,1,2,0:T(8,128)(2,1)}, u32[]{:S(2)}, u32[]{:S(2)}) %collective-permute-start.2) | collective-permute-done | bytes 811040 | tf_op jit(solution)/shard_map/ppermute | solution.py:20
  96.2 2.2 %constant_dynamic-update-slice_fusion = bf16[2,1056,6,128]{3,1,2,0:T(8,128)(2,1)} fusion(bf16[2,1056,6,128]{3,1,2,0:T(8,128)(2,1)} %constant_dynamic-update-slice_fusion.1, bf16[2,264,6,128]{3,1,2,0:T(8,128)(2,1)} %collective-permute-done.2, s32[]{:T(128)S(6)} %select_n.45), kind=kLoop, calls=%fused_computation.34 | loop fusion | bytes 1622020 | tf_op jit(solution)/shard_map/dynamic_update_slice | solution.py:18
  98.4 17.1 %while.18 = (s32[]{:T(128)}, f32[6,264]{1,0:T(8,128)S(1)}, f32[6,264]{1,0:T(8,128)S(1)}, f32[6,264,128]{2,1,0:T(8,128)S(1)}, bf16[2,1056,6,128]{3,1,2,0:T(8,128)...) while((s32[]{:T(128)}, f32[6,264]{1,0:T(8,128)S(1)}, ...), condition=%wide.region_3.4_spmd.clone, body=%wide.region_0.3_spmd.clone.sunk | while | flops 218067712 | bytes 7958207 | solution.py:67
  98.4 1.7 %bitcast_reduce_fusion.2 = (f32[6,264]{1,0:T(8,128)S(1)}, f32[6,264,264]{2,1,0:T(8,128)S(1)}) fusion(bf16[264,6,128]{2,0,1:T(8,128)(2,1)} %get-tuple-element.225, bf16[2,1056,6,128]{3,1,2,0:T(8,128)(2,1)} %get-tuple-element.224, s32[]{:T(128)S(6)} %select_n.48), kind=kOutput, calls=%fused_computation.1.clone.1 | convolution fusion | flops 107887824 | bytes 2490052 | tf_op jit(solution)/shard_map/while/body/eval_jaxpr/qhd,khd->hqk/dot_general | solution.py:28
  100.2 0.4 fusion.26
  100.6 2.0 %convolution_add_fusion.2 = f32[6,264,128]{2,1,0:T(8,128)S(1)} fusion(f32[6,264,264]{2,1,0:T(8,128)S(1)} %get-tuple-element.195, f32[6,264]{1,0:T(8,128)S(1)} %select_maximum_fusion.2, f32[6,264,128]{2,1,0:T(8,128)S(1)} %get-tuple-element.212, bf16[2,1056,6,128]{3,1,2,0:T(8,128)(2,1)} %get-tuple-element.224, s32[]{:T(128)S(6)} %add.89, ...), kind=kOutput, calls=%fused_computation.5.clone.1 | convolution fusion | flops 108915840 | bytes 3712905 | tf_op jit(solution)/shard_map/while/body/eval_jaxpr/hqk,khd->hqd/dot_general | solution.py:35
  102.7 1.7 %bitcast_reduce_fusion.2 = (f32[6,264]{1,0:T(8,128)S(1)}, f32[6,264,264]{2,1,0:T(8,128)S(1)}) fusion(bf16[264,6,128]{2,0,1:T(8,128)(2,1)} %get-tuple-element.225, bf16[2,1056,6,128]{3,1,2,0:T(8,128)(2,1)} %get-tuple-element.224, s32[]{:T(128)S(6)} %select_n.48), kind=kOutput, calls=%fused_computation.1.clone.1 | convolution fusion | flops 107887824 | bytes 2490052 | tf_op jit(solution)/shard_map/while/body/eval_jaxpr/qhd,khd->hqk/dot_general | solution.py:28
  104.4 0.4 fusion.26
  104.9 2.0 %convolution_add_fusion.2 = f32[6,264,128]{2,1,0:T(8,128)S(1)} fusion(f32[6,264,264]{2,1,0:T(8,128)S(1)} %get-tuple-element.195, f32[6,264]{1,0:T(8,128)S(1)} %select_maximum_fusion.2, f32[6,264,128]{2,1,0:T(8,128)S(1)} %get-tuple-element.212, bf16[2,1056,6,128]{3,1,2,0:T(8,128)(2,1)} %get-tuple-element.224, s32[]{:T(128)S(6)} %add.89, ...), kind=kOutput, calls=%fused_computation.5.clone.1 | convolution fusion | flops 108915840 | bytes 3712905 | tf_op jit(solution)/shard_map/while/body/eval_jaxpr/hqk,khd->hqd/dot_general | solution.py:35
  107.0 1.7 %bitcast_reduce_fusion.2 = (f32[6,264]{1,0:T(8,128)S(1)}, f32[6,264,264]{2,1,0:T(8,128)S(1)}) fusion(bf16[264,6,128]{2,0,1:T(8,128)(2,1)} %get-tuple-element.225, bf16[2,1056,6,128]{3,1,2,0:T(8,128)(2,1)} %get-tuple-element.224, s32[]{:T(128)S(6)} %select_n.48), kind=kOutput, calls=%fused_computation.1.clone.1 | convolution fusion | flops 107887824 | bytes 2490052 | tf_op jit(solution)/shard_map/while/body/eval_jaxpr/qhd,khd->hqk/dot_general | solution.py:28
  108.7 0.4 fusion.26
  109.2 2.0 %convolution_add_fusion.2 = f32[6,264,128]{2,1,0:T(8,128)S(1)} fusion(f32[6,264,264]{2,1,0:T(8,128)S(1)} %get-tuple-element.195, f32[6,264]{1,0:T(8,128)S(1)} %select_maximum_fusion.2, f32[6,264,128]{2,1,0:T(8,128)S(1)} %get-tuple-element.212, bf16[2,1056,6,128]{3,1,2,0:T(8,128)(2,1)} %get-tuple-element.224, s32[]{:T(128)S(6)} %add.89, ...), kind=kOutput, calls=%fused_computation.5.clone.1 | convolution fusion | flops 108915840 | bytes 3712905 | tf_op jit(solution)/shard_map/while/body/eval_jaxpr/hqk,khd->hqd/dot_general | solution.py:35
  111.2 1.7 %bitcast_reduce_fusion.2 = (f32[6,264]{1,0:T(8,128)S(1)}, f32[6,264,264]{2,1,0:T(8,128)S(1)}) fusion(bf16[264,6,128]{2,0,1:T(8,128)(2,1)} %get-tuple-element.225, bf16[2,1056,6,128]{3,1,2,0:T(8,128)(2,1)} %get-tuple-element.224, s32[]{:T(128)S(6)} %select_n.48), kind=kOutput, calls=%fused_computation.1.clone.1 | convolution fusion | flops 107887824 | bytes 2490052 | tf_op jit(solution)/shard_map/while/body/eval_jaxpr/qhd,khd->hqk/dot_general | solution.py:28
  113.0 0.4 fusion.26
  113.5 2.0 %convolution_add_fusion.2 = f32[6,264,128]{2,1,0:T(8,128)S(1)} fusion(f32[6,264,264]{2,1,0:T(8,128)S(1)} %get-tuple-element.195, f32[6,264]{1,0:T(8,128)S(1)} %select_maximum_fusion.2, f32[6,264,128]{2,1,0:T(8,128)S(1)} %get-tuple-element.212, bf16[2,1056,6,128]{3,1,2,0:T(8,128)(2,1)} %get-tuple-element.224, s32[]{:T(128)S(6)} %add.89, ...), kind=kOutput, calls=%fused_computation.5.clone.1 | convolution fusion | flops 108915840 | bytes 3712905 | tf_op jit(solution)/shard_map/while/body/eval_jaxpr/hqk,khd->hqd/dot_general | solution.py:35
  115.5 0.0 copy-start.1
  115.5 0.1 copy.24
  115.7 0.4 fusion.14
  116.0 0.6 slice_bitcast_fusion.1
  116.6 3.3 %all-to-all-start.3 = ((bf16[8,1,6,128]{3,2,1,0:T(8,128)(2,1)}), bf16[8,1,6,128]{3,2,1,0:T(8,128)(2,1)S(1)}, u32[]{:S(2)}, u32[]{:S(2)}) async-start(bf16[8,1,6,128]{3,2,1,0:T(8,128)(2,1)} %slice_bitcast_fusion.1), calls=%async_computation.3 | async-start | bytes 32768 | tf_op jit(solution)/shard_map/all_to_all | solution.py:88
  119.9 0.8 slice_bitcast_fusion
  120.7 3.0 %all-to-all-done.3 = bf16[8,1,6,128]{3,2,1,0:T(8,128)(2,1)S(1)} async-done(((bf16[8,1,6,128]{3,2,1,0:T(8,128)(2,1)}), bf16[8,1,6,128]{3,2,1,0:T(8,128)(2,1)S(1)}, u32[]{:S(2)}, u32[]{:S(2)}) %all-to-all-start.3) | async-done | bytes 12320 | tf_op jit(solution)/shard_map/all_to_all | solution.py:88
  123.7 3.5 %all-to-all-start.2 = ((bf16[256,1,6,128]{3,2,1,0:T(8,128)(2,1)}), bf16[256,1,6,128]{3,2,1,0:T(8,128)(2,1)S(1)}, u32[]{:S(2)}, u32[]{:S(2)}) async-start(bf16[256,1,6,128]{3,2,1,0:T(8,128)(2,1)} %slice_bitcast_fusion), calls=%async_computation.2 | async-start | bytes 1048576 | tf_op jit(solution)/shard_map/all_to_all | solution.py:87
  127.2 0.0 copy-done.1
  127.3 0.6 multiply_convert_fusion.1
  127.9 8.1 %all-to-all-done.2 = bf16[256,1,6,128]{3,2,1,0:T(8,128)(2,1)S(1)} async-done(((bf16[256,1,6,128]{3,2,1,0:T(8,128)(2,1)}), bf16[256,1,6,128]{3,2,1,0:T(8,128)(2,1)S(1)}, u32[]{:S(2)}, u32[]{:S(2)}) %all-to-all-start.2) | async-done | bytes 393248 | tf_op jit(solution)/shard_map/all_to_all | solution.py:87
  136.0 0.1 copy_bitcast_fusion
  136.1 0.2 reshape.41
  136.3 0.8 multiply_convert_fusion
  (20 shorter events, 0.2 us)
Async XLA Ops:
  2.1 8.6 %all-to-all-start.1 = ((bf16[3,2,4,6,128]{4,1,3,0,2:T(2,128)(2,1)}), bf16[3,2,4,6,128]{4,1,3,0,2:T(2,128)(2,1)S(1)}, u32[]{:S(2)}, u32[]{:S(2)}) async-start(bf16[3,2,4,6,128]{4,1,3,0,2:T(2,128)(2,1)} %copy.22), calls=%async_computation.1 | async-start | bytes 73728 | tf_op jit(solution)/shard_map/all_to_all | solution.py:83
  10.6 19.3 %all-to-all-start = ((bf16[3,64,4,6,128]{4,1,3,0,2:T(8,128)(2,1)}), bf16[3,64,4,6,128]{4,1,3,0,2:T(8,128)(2,1)S(1)}, u32[]{:S(2)}, u32[]{:S(2)}) async-start(bf16[3,64,4,6,128]{4,1,3,0,2:T(8,128)(2,1)} %copy.20), calls=%async_computation | async-start | bytes 2359296 | tf_op jit(solution)/shard_map/all_to_all | solution.py:82
  33.3 21.9 %collective-permute-start = (bf16[2,264,6,128]{3,1,2,0:T(8,128)(2,1)S(1)}, bf16[2,264,6,128]{3,1,2,0:T(8,128)(2,1)S(1)}, u32[]{:S(2)}, u32[]{:S(2)}) collective-permute-start(bf16[2,264,6,128]{3,1,2,0:T(8,128)(2,1)S(1)} %get-tuple-element.150), channel_id=1, source_target_pairs={{0,4},{4,8},{8,12},{12,0},{1,5},{5,9},{9,13},{13,1},{2,6},{6,10},{... | collective-permute-start | bytes 2433032 | tf_op jit(solution)/shard_map/ppermute | solution.py:20
  55.2 20.8 %collective-permute-start.1 = (bf16[2,264,6,128]{3,1,2,0:T(8,128)(2,1)S(1)}, bf16[2,264,6,128]{3,1,2,0:T(8,128)(2,1)}, u32[]{:S(2)}, u32[]{:S(2)}) collective-permute-start(bf16[2,264,6,128]{3,1,2,0:T(8,128)(2,1)S(1)} %collective-permute-done), channel_id=1, source_target_pairs={{0,4},{4,8},{8,12},{12,0},{1,5},{5,9},{9,13},{13,1},{2,6},{6,10},{... | collective-permute-start | bytes 2433032 | tf_op jit(solution)/shard_map/ppermute | solution.py:20
  76.0 20.2 %collective-permute-start.2 = (bf16[2,264,6,128]{3,1,2,0:T(8,128)(2,1)}, bf16[2,264,6,128]{3,1,2,0:T(8,128)(2,1)}, u32[]{:S(2)}, u32[]{:S(2)}) collective-permute-start(bf16[2,264,6,128]{3,1,2,0:T(8,128)(2,1)} %collective-permute-done.1), channel_id=1, source_target_pairs={{0,4},{4,8},{8,12},{12,0},{1,5},{5,9},{9,13},{13,1},{2,6},{6,10},{... | collective-permute-start | bytes 2433032 | tf_op jit(solution)/shard_map/ppermute | solution.py:20
  115.5 11.7 %copy-start.1 = (f32[3072]{0:T(1024)S(1)}, f32[3072]{0:T(1024)}, u32[]{:S(2)}) copy-start(f32[3072]{0:T(1024)} %param.9) | copy-start | bytes 36868
  116.6 7.1 %all-to-all-start.3 = ((bf16[8,1,6,128]{3,2,1,0:T(8,128)(2,1)}), bf16[8,1,6,128]{3,2,1,0:T(8,128)(2,1)S(1)}, u32[]{:S(2)}, u32[]{:S(2)}) async-start(bf16[8,1,6,128]{3,2,1,0:T(8,128)(2,1)} %slice_bitcast_fusion.1), calls=%async_computation.3 | async-start | bytes 32768 | tf_op jit(solution)/shard_map/all_to_all | solution.py:88
  120.7 15.6 %copy-start = (f32[3072]{0:T(1024)S(1)}, f32[3072]{0:T(1024)}, u32[]{:S(2)}) copy-start(f32[3072]{0:T(1024)} %param.8) | copy-start | bytes 36868
  123.7 12.3 %all-to-all-start.2 = ((bf16[256,1,6,128]{3,2,1,0:T(8,128)(2,1)}), bf16[256,1,6,128]{3,2,1,0:T(8,128)(2,1)S(1)}, u32[]{:S(2)}, u32[]{:S(2)}) async-start(bf16[256,1,6,128]{3,2,1,0:T(8,128)(2,1)} %slice_bitcast_fusion), calls=%async_computation.2 | async-start | bytes 1048576 | tf_op jit(solution)/shard_map/all_to_all | solution.py:87
